TPU v7x, 32 devices: a 4x4x1 block of a 4x4x8 slice. The times are simulated.
32 devices in a mesh: dp: 1 (over z), sp: 32 (over y, x, core).
Axes of the slice: x: 4, y: 4, z: 1, core: 2. Of those that a mesh axis runs over, the one named last changes fastest.
The devices are a block of a 4x4x8 slice.
Arguments:
- latents: bfloat16 [6, 64, 256, 384], P('dp', 'sp')
- text_ctx: bfloat16 [6, 120, 384], P('dp')
- modulation: float32 [6, 6, 384], P('dp')
- pos_temporal: float32 [64, 384], replicated
- w_qkv_spatial: bfloat16 [3, 6, 64, 384], replicated
- w_out_spatial: bfloat16 [6, 64, 384], replicated
- w_qkv_temporal: bfloat16 [3, 6, 64, 384], replicated
- w_out_temporal: bfloat16 [6, 64, 384], replicated
- w_query_cross: bfloat16 [6, 64, 384], replicated
- w_kv_cross: bfloat16 [2, 6, 64, 384], replicated
- w_out_cross: bfloat16 [6, 64, 384], replicated
- w_mlp_in: bfloat16 [384, 1536], replicated
- w_mlp_out: bfloat16 [1536, 384], replicated
Outputs:
- output: bfloat16 [6, 64, 256, 384], P('dp', 'sp')
All inputs are finite; a program needn't handle non-finite values.
Results may differ from a plain program's by a relative error of at most 0.014326.
Values are sent between devices in bfloat16 or wider.
A program may use at most 768 MiB of HBM per device.

v0:
```python
import functools

import jax
import jax.numpy as jnp
from jax import lax
from jax.experimental import pallas as pl
from jax.experimental.pallas import tpu as pltpu
from jax.sharding import PartitionSpec as P

LN_EPS = 1e-6
LOG2E = 1.4426950408889634
F32 = jnp.float32
BF16 = jnp.bfloat16
MESH = pl.DeviceIdType.MESH
WEIGHTS = ('w_qkv_s', 'w_out_s', 'w_qkv_t', 'w_out_t', 'w_q_c', 'w_kv_c', 'w_out_c', 'w_in', 'w_up')


def mm(lhs, rhs):
    return lax.dot_general(lhs, rhs, (((1,), (0,)), ((), ())), preferred_element_type=F32)


def mm_nt(lhs, rhs):
    return lax.dot_general(lhs, rhs, (((1,), (1,)), ((), ())), preferred_element_type=F32)


def mm_tn(lhs, rhs):
    return lax.dot_general(lhs, rhs, (((0,), (0,)), ((), ())), preferred_element_type=F32)


def layer_norm(acts):
    centered = acts - jnp.mean(acts, axis=-1, keepdims=True)
    return centered * lax.rsqrt(jnp.mean(centered * centered, axis=-1, keepdims=True) + LN_EPS)


def probs_t(scores_t, scale):
    shifted = (scores_t - jnp.max(scores_t, axis=0, keepdims=True)) * (scale * LOG2E)
    weights = jnp.exp2(shifted)
    return weights * (1.0 / jnp.sum(weights, axis=0, keepdims=True))


def padded_head(q_t, head, dim):
    rows = q_t[head * dim:(head + 1) * dim]
    zeros = jnp.zeros_like(rows)
    return jnp.concatenate([rows, zeros] if head % 2 == 0 else [zeros, rows], axis=0)


def head_pair(k, head, dim):
    lo = (head // 2) * 2 * dim
    return k[:, lo:lo + 2 * dim]


def project_qkv(acts, w_ref, width):
    q_t = mm_nt(w_ref[0:width], acts).astype(BF16)
    v_t = mm_nt(w_ref[2 * width:3 * width], acts).astype(BF16)
    k = mm_nt(acts, w_ref[width:2 * width]).astype(BF16)
    return q_t, k, v_t


def block_kernel(cfg, x_hbm, ctx_hbm, mod_hbm, pos_hbm, *rest):
    n, B, F, S, C, H, D, L = cfg
    PP = S // n
    T = F * n
    R = F * PP
    NW = len(WEIGHTS)
    w_hbm = rest[:NW]
    y_hbm = rest[NW]
    (xb, ctxb, modb, posb) = rest[NW + 1:NW + 5]
    wv = rest[NW + 5:2 * NW + 5]
    (sb1, rb1, sb2, rb2, zf, yb, kc, vc, lsem, xsem, ysem, ssem1, rsem1, ssem2, rsem2) = rest[2 * NW + 5:]
    w_qkv_s, w_out_s, w_qkv_t, w_out_t, w_q_c, w_kv_c, w_out_c, w_in, w_up = wv
    scale = D ** -0.5
    me = lax.axis_index('sp')

    def x_copy(b):
        return pltpu.make_async_copy(x_hbm.at[b], xb.at[b], xsem.at[b])

    loads = [pltpu.make_async_copy(src, dst, lsem.at[i]) for i, (src, dst) in enumerate(
        zip((ctx_hbm, mod_hbm, pos_hbm) + tuple(w_hbm), (ctxb, modb, posb) + tuple(wv)))]
    x_copy(0).start()
    loads[1].start()
    loads[3].start()
    loads[4].start()
    for b in range(1, B):
        x_copy(b).start()
    for i in (0, 2, 5, 6, 7, 8, 9, 10, 11):
        loads[i].start()

    barrier = pltpu.get_barrier_semaphore()

    @pl.loop(1, n)
    def _(j):
        pl.semaphore_signal(barrier, inc=1, device_id={'sp': lax.rem(me + j, n)}, device_id_type=MESH)

    pl.semaphore_wait(barrier, n - 1)

    def send_all(b, sbuf, rbuf, ssem, rsem):
        rbuf[b, me] = sbuf[b, me]

        @pl.loop(1, n)
        def _(j):
            peer = lax.rem(me + j, n)
            pltpu.make_async_remote_copy(
                src_ref=sbuf.at[b, peer], dst_ref=rbuf.at[b, me], send_sem=ssem.at[b], recv_sem=rsem.at[b],
                device_id={'sp': peer}, device_id_type=MESH).start()

    def whole(b, sbuf, rbuf, ssem, rsem):
        return pltpu.make_async_remote_copy(
            src_ref=sbuf.at[b, pl.ds(0, n - 1)], dst_ref=rbuf.at[b, pl.ds(0, n - 1)], send_sem=ssem.at[b],
            recv_sem=rsem.at[b], device_id={'sp': me}, device_id_type=MESH)

    loads[1].wait()
    loads[3].wait()
    loads[4].wait()

    @pl.loop(0, B)
    def _(b):
        x_copy(b).wait()
        mod = modb[b]
        outs = []
        for f in range(F):
            lat = xb[b, f].astype(F32)
            acts = (layer_norm(lat) * (1.0 + mod[1:2]) + mod[0:1]).astype(BF16)
            q_t, k, v_t = project_qkv(acts, w_qkv_s, C)
            heads = []
            for h in range(H):
                s_t = mm(head_pair(k, h, D), padded_head(q_t, h, D))
                p_t = probs_t(s_t, scale).astype(BF16)
                heads.append(mm(v_t[h * D:(h + 1) * D], p_t).astype(BF16))
            branch = mm_tn(jnp.concatenate(heads, axis=0), w_out_s[...])
            outs.append((lat + mod[2:3] * branch).reshape(n, PP, C))
        sb1[b] = jnp.concatenate(outs, axis=1).astype(BF16)
        send_all(b, sb1, rb1, ssem1, rsem1)

    loads[0].wait()
    loads[8].wait()

    @pl.loop(0, B)
    def _(b):
        ctx = ctxb[b]
        kc[b] = mm_nt(ctx, w_kv_c[0:C]).astype(BF16)
        vc[b] = mm_nt(ctx, w_kv_c[C:2 * C]).astype(BF16)

    loads[2].wait()
    loads[5].wait()
    loads[6].wait()
    group = 256 // T if T <= 128 else 1
    group = min(group, PP)

    @pl.loop(0, B)
    def _(b):
        whole(b, sb1, rb1, ssem1, rsem1).wait_recv()
        mod = modb[b]
        pos = posb[...]
        low = lax.broadcasted_iota(jnp.int32, (T, 2 * T), 1) < T
        arrived = rb1[b].astype(F32).reshape(n * R, C)
        for c in range(C // 128):
            zf[c] = arrived[:, c * 128:(c + 1) * 128]
        for g in range(PP // group):
            tokens = jnp.concatenate([jnp.concatenate(
                [zf[c, pl.ds(g * group + i, T, PP), :] for c in range(C // 128)], axis=1) for i in range(group)], axis=0)
            acts = (tokens + jnp.concatenate([pos] * group, axis=0)).astype(BF16)
            q_t, k, v_t = project_qkv(acts, w_qkv_t, C)
            heads = []
            for h in range(H):
                q_h = padded_head(q_t, h, D)
                k_h = head_pair(k, h, D)
                v_h = v_t[h * D:(h + 1) * D]
                parts = []
                for i in range(group // 2):
                    lanes = slice(i * 2 * T, (i + 1) * 2 * T)
                    s_t = mm(k_h[lanes], q_h[:, lanes])
                    p_t = probs_t(jnp.where(low, s_t[0:T], s_t[T:2 * T]), scale)
                    p_t = jnp.concatenate([jnp.where(low, p_t, 0.0), jnp.where(low, 0.0, p_t)], axis=0).astype(BF16)
                    parts.append(mm(v_h[:, lanes], p_t).astype(BF16))
                heads.append(jnp.concatenate(parts, axis=1))
            branch = mm_tn(jnp.concatenate(heads, axis=0), w_out_t[...])
            after = tokens + mod[2:3] * branch
            for i in range(group):
                for c in range(C // 128):
                    zf[c, pl.ds(g * group + i, T, PP), :] = after[i * T:(i + 1) * T, c * 128:(c + 1) * 128]
        leaving = jnp.concatenate([zf[c] for c in range(C // 128)], axis=1)
        sb2[b] = leaving.astype(BF16).reshape(n, R, C)
        send_all(b, sb2, rb2, ssem2, rsem2)

    for i in (7, 9, 10, 11):
        loads[i].wait()

    @pl.loop(0, B)
    def _(b):
        whole(b, sb2, rb2, ssem2, rsem2).wait_recv()
        mod = modb[b]
        k_all = kc[b]
        v_all = vc[b]
        for f in range(F):
            hid_f = rb2[b].astype(F32)[:, f * PP:(f + 1) * PP, :].reshape(S, C)
            q_t = mm_nt(w_q_c[...], hid_f.astype(BF16)).astype(BF16)
            heads = []
            for h in range(H):
                s_t = mm(head_pair(k_all, h, D), padded_head(q_t, h, D))
                p_t = probs_t(s_t, scale).astype(BF16)
                lo = (h // 2) * 2 * D
                o_t = mm_tn(v_all[:, lo:lo + 2 * D], p_t)
                heads.append(o_t[(h % 2) * D:(h % 2 + 1) * D].astype(BF16))
            branch = mm_tn(jnp.concatenate(heads, axis=0), w_out_c[...])
            cross = (hid_f + branch).astype(BF16).astype(F32)
            normed = (layer_norm(cross) * (1.0 + mod[4:5]) + mod[3:4]).astype(BF16)
            grown = jax.nn.gelu(mm(normed, w_in[...]), approximate=True).astype(BF16)
            yb[b, f] = (cross + mod[5:6] * mm(grown, w_up[...])).astype(BF16)
        pltpu.make_async_copy(yb.at[b], y_hbm.at[b], ysem.at[b]).start()

    @pl.loop(0, B)
    def _(b):
        pltpu.make_async_copy(yb.at[b], y_hbm.at[b], ysem.at[b]).wait()
        whole(b, sb1, rb1, ssem1, rsem1).wait_send()
        whole(b, sb2, rb2, ssem2, rsem2).wait_send()


def solution(mesh):
    n = mesh.shape['sp']
    act_spec = P('dp', 'sp', None, None)
    row_spec = P('dp', None, None)
    rep = [P(*[None] * k) for k in range(5)]
    in_specs = (act_spec, row_spec, row_spec, rep[2], rep[4], rep[3], rep[4], rep[3], rep[3], rep[4], rep[3], rep[2], rep[2])

    def local_block(latents, text_ctx, modulation, pos_temporal, w_qkv_spatial, w_out_spatial, w_qkv_temporal, w_out_temporal, w_query_cross, w_kv_cross, w_out_cross, w_mlp_in, w_mlp_out):
        B, F, S, C = latents.shape
        H, D, _ = w_out_spatial.shape
        L = text_ctx.shape[1]
        weights = [w.reshape(-1, w.shape[-1]) for w in (w_qkv_spatial, w_out_spatial, w_qkv_temporal, w_out_temporal, w_query_cross, w_kv_cross, w_out_cross, w_mlp_in, w_mlp_out)]
        args = [latents, text_ctx, modulation, pos_temporal] + weights
        R = F * (S // n)
        chunk = pltpu.VMEM((B, n, R, C), BF16)
        return pl.pallas_call(
            functools.partial(block_kernel, (n, B, F, S, C, H, D, L)),
            out_shape=jax.ShapeDtypeStruct(latents.shape, BF16),
            in_specs=[pl.BlockSpec(memory_space=pl.ANY)] * len(args),
            out_specs=pl.BlockSpec(memory_space=pl.ANY),
            scratch_shapes=[pltpu.VMEM(a.shape, a.dtype) for a in args] + [
                chunk, chunk, chunk, chunk,
                pltpu.VMEM((C // 128, n * R, 128), F32),
                pltpu.VMEM(latents.shape, BF16),
                pltpu.VMEM((B, L, C), BF16),
                pltpu.VMEM((B, L, C), BF16),
                pltpu.SemaphoreType.DMA((len(args) - 1,)),
                pltpu.SemaphoreType.DMA((B,)),
                pltpu.SemaphoreType.DMA((B,)),
                pltpu.SemaphoreType.DMA((B,)),
                pltpu.SemaphoreType.DMA((B,)),
                pltpu.SemaphoreType.DMA((B,)),
                pltpu.SemaphoreType.DMA((B,)),
            ],
            compiler_params=pltpu.CompilerParams(collective_id=0, has_side_effects=True, vmem_limit_bytes=60 * 1024 * 1024),
            name='st_block',
        )(*args)

    return jax.shard_map(local_block, mesh=mesh, in_specs=in_specs, out_specs=act_spec, check_vma=False)
```

profile of v0, /device:TPU:97, one launch (start us, length us, event | category | flops | bytes accessed | tf_op | source)
XLA Modules:
  0.0 110.4 jit_solution(17700004949395327049)
XLA Ops:
  0.0 107.1 %st_block.1 = bf16[6,2,256,384]{3,2,1,0:T(8,128)(2,1)} custom-call(bf16[6,2,256,384]{3,2,1,0:T(8,128)(2,1)} %x_hbm.1, bf16[6,120,384]{2,1,0:T(8,128)(2,1)} %ctx_hbm.1, f32[6,6,384]{2,1,0:T(8,128)} %mod_hbm.1, f32[64,384]{1,0:T(8,128)} %pos_hbm.1, bf16[1152,384]{1,0:T(8,128)(2,1)} %bitcast.7, bf16[384,384]{1,0:T(8,128)(2,1)} %bitcast.10, ...), custom_call_target="tpu_custom_call" | custom-call | tf_op jit(solution)/shard_map/st_block/pallas_call | solution.py:233
  107.1 3.3 %copy.15 = bf16[6,2,256,384]{3,2,1,0:T(8,128)(2,1)} copy(bf16[6,2,256,384]{3,2,1,0:T(8,128)(2,1)} %st_block.1) | data formatting | bytes 4718592
where the time goes:
time: 111 us; the launch traced here: 110 us
  Pallas kernels  107 us (96%)
  local copies, waits for them, and re-layouts  3.31 us (3%)
    pallas_call x1, Pallas kernels, local_block(): pl.pallas_call(functools.partial(block_kernel, (n, B, F, S, C, H, D, L)),...  107 us
    unnamed x1, local copies, waits for them, and re-layouts  3.31 us

commit v1 on v0

v1 whole, which is shorter than its diff:
```python
import functools

import jax
import jax.numpy as jnp
from jax import lax
from jax.experimental import pallas as pl
from jax.experimental.pallas import tpu as pltpu
from jax.sharding import PartitionSpec as P

LN_EPS = 1e-6
LOG2E = 1.4426950408889634
GELU_A = 0.7978845608028654
GELU_B = 0.044715 * GELU_A
F32 = jnp.float32
BF16 = jnp.bfloat16
MESH = pl.DeviceIdType.MESH
DEPTH = 4
WEIGHTS = ('w_qkv_s', 'w_out_s', 'w_qkv_t', 'w_out_t', 'w_q_c', 'w_kv_c', 'w_out_c', 'w_in', 'w_up')


def mm(lhs, rhs):
    return lax.dot_general(lhs, rhs, (((1,), (0,)), ((), ())), preferred_element_type=F32)


def mm_nt(lhs, rhs):
    return lax.dot_general(lhs, rhs, (((1,), (1,)), ((), ())), preferred_element_type=F32)


def mm_tn(lhs, rhs):
    return lax.dot_general(lhs, rhs, (((0,), (0,)), ((), ())), preferred_element_type=F32)


def gelu(acts):
    inner = acts * (GELU_A + GELU_B * (acts * acts))
    half = 0.5 * acts
    return half + half * jnp.tanh(inner)


def layer_norm(acts):
    centered = acts - jnp.mean(acts, axis=-1, keepdims=True)
    return centered * lax.rsqrt(jnp.mean(centered * centered, axis=-1, keepdims=True) + LN_EPS)


def padded_head(q_ref, head, dim, lanes):
    rows = q_ref[head * dim:(head + 1) * dim, lanes]
    zeros = jnp.zeros_like(rows)
    return jnp.concatenate([rows, zeros] if head % 2 == 0 else [zeros, rows], axis=0)


def pair_lanes(head, dim):
    lo = (head // 2) * 2 * dim
    return slice(lo, lo + 2 * dim)


def weights_t(scores_t, scale):
    top = jnp.max(scores_t, axis=0, keepdims=True)
    weights = jnp.exp2((scores_t - top) * (scale * LOG2E))
    return weights, 1.0 / jnp.sum(weights, axis=0, keepdims=True)


def staged(units, score, soften, combine):
    for i in range(len(units) + 2):
        if i < len(units):
            score(i % DEPTH, *units[i])
        if 0 <= i - 1 < len(units):
            soften((i - 1) % DEPTH, *units[i - 1])
        if 0 <= i - 2 < len(units):
            combine((i - 2) % DEPTH, *units[i - 2])


def block_kernel(cfg, x_hbm, ctx_hbm, mod_hbm, pos_hbm, *rest):
    n, B, F, S, C, H, D, L = cfg
    PP = S // n
    T = F * n
    R = F * PP
    NW = len(WEIGHTS)
    w_hbm = rest[:NW]
    y_hbm = rest[NW]
    (xb, ctxb, modb, posb) = rest[NW + 1:NW + 5]
    wv = rest[NW + 5:2 * NW + 5]
    (sb1, rb1, sb2, rb2, zf, yb, kc, vc, qs, ks, vs, at, sc, pc, rs, tok, act, grown, lsem, xsem, ysem, ssem1, rsem1, ssem2, rsem2) = rest[2 * NW + 5:]
    w_qkv_s, w_out_s, w_qkv_t, w_out_t, w_q_c, w_kv_c, w_out_c, w_in, w_up = wv
    scale = D ** -0.5
    me = lax.axis_index('sp')

    def x_copy(b):
        return pltpu.make_async_copy(x_hbm.at[b], xb.at[b], xsem.at[b])

    loads = [pltpu.make_async_copy(src, dst, lsem.at[i]) for i, (src, dst) in enumerate(
        zip((ctx_hbm, mod_hbm, pos_hbm) + tuple(w_hbm), (ctxb, modb, posb) + tuple(wv)))]
    x_copy(0).start()
    loads[1].start()
    loads[3].start()
    loads[4].start()
    for b in range(1, B):
        x_copy(b).start()
    for i in (0, 2, 5, 6, 7, 8, 9, 10, 11):
        loads[i].start()

    barrier = pltpu.get_barrier_semaphore()

    @pl.loop(1, n)
    def _(j):
        pl.semaphore_signal(barrier, inc=1, device_id={'sp': lax.rem(me + j, n)}, device_id_type=MESH)

    pl.semaphore_wait(barrier, n - 1)

    def send_all(b, sbuf, rbuf, ssem, rsem):
        rbuf[b, me] = sbuf[b, me]

        @pl.loop(1, n)
        def _(j):
            peer = lax.rem(me + j, n)
            pltpu.make_async_remote_copy(
                src_ref=sbuf.at[b, peer], dst_ref=rbuf.at[b, me], send_sem=ssem.at[b], recv_sem=rsem.at[b],
                device_id={'sp': peer}, device_id_type=MESH).start()

    def whole(b, sbuf, rbuf, ssem, rsem):
        return pltpu.make_async_remote_copy(
            src_ref=sbuf.at[b, pl.ds(0, n - 1)], dst_ref=rbuf.at[b, pl.ds(0, n - 1)], send_sem=ssem.at[b],
            recv_sem=rsem.at[b], device_id={'sp': me}, device_id_type=MESH)

    def project_qkv(i, w_ref):
        acts = act[i]
        qs[i] = mm_nt(w_ref[0:C], acts).astype(BF16)
        ks[i] = mm_nt(acts, w_ref[C:2 * C]).astype(BF16)
        vs[i] = mm_nt(w_ref[2 * C:3 * C], acts).astype(BF16)

    every = slice(None)

    loads[1].wait()
    loads[3].wait()
    loads[4].wait()

    def spatial_score(slot, f, h):
        sc[slot] = mm(ks[f, :, pair_lanes(h, D)], padded_head(qs.at[f], h, D, every))

    def spatial_soften(slot, f, h):
        weights, inverse = weights_t(sc[slot], scale)
        pc[slot] = weights.astype(BF16)
        rs[slot] = jnp.broadcast_to(inverse, rs.shape[1:])

    def spatial_combine(slot, f, h):
        mixed = mm(vs[f, h * D:(h + 1) * D], pc[slot]) * rs[slot, 0:1]
        at[h * D:(h + 1) * D, f * S:(f + 1) * S] = mixed.astype(BF16)

    units = [(f, h) for f in range(F) for h in range(H)]

    @pl.loop(0, B)
    def _(b):
        x_copy(b).wait()
        mod = modb[b]
        for f in range(F):
            act[f] = (layer_norm(xb[b, f].astype(F32)) * (1.0 + mod[1:2]) + mod[0:1]).astype(BF16)
            project_qkv(f, w_qkv_s)
        staged(units, spatial_score, spatial_soften, spatial_combine)
        branch = mm_tn(at[...], w_out_s[...])
        outs = [(xb[b, f].astype(F32) + mod[2:3] * branch[f * S:(f + 1) * S]).reshape(n, PP, C) for f in range(F)]
        sb1[b] = jnp.concatenate(outs, axis=1).astype(BF16)
        send_all(b, sb1, rb1, ssem1, rsem1)

    loads[0].wait()
    loads[8].wait()

    @pl.loop(0, B)
    def _(b):
        ctx = jnp.concatenate([ctxb[b].astype(F32), jnp.zeros((kc.shape[1] - L, C), F32)], axis=0).astype(BF16)
        kc[b] = mm_nt(ctx, w_kv_c[0:C]).astype(BF16)
        vc[b] = mm_nt(w_kv_c[C:2 * C], ctx).astype(BF16)

    loads[2].wait()
    loads[5].wait()
    loads[6].wait()
    G = S // T
    low = lax.broadcasted_iota(jnp.int32, (T, 2 * T), 1) < T
    pairs = [slice(i * 2 * T, (i + 1) * 2 * T) for i in range(G // 2)]

    def temporal_score(slot, g, h):
        for lanes in pairs:
            s_t = mm(ks[g, lanes, pair_lanes(h, D)], padded_head(qs.at[g], h, D, lanes))
            sc[slot, 0:T, lanes] = jnp.where(low, s_t[0:T], s_t[T:2 * T])

    def temporal_soften(slot, g, h):
        for lanes in pairs:
            weights, inverse = weights_t(sc[slot, 0:T, lanes], scale)
            pc[slot, 0:T, lanes] = jnp.where(low, weights, 0.0).astype(BF16)
            pc[slot, T:2 * T, lanes] = jnp.where(low, 0.0, weights).astype(BF16)
            rs[slot, :, lanes] = jnp.broadcast_to(inverse, (rs.shape[1], 2 * T))

    def temporal_combine(slot, g, h):
        for i, lanes in enumerate(pairs):
            mixed = mm(vs[g, h * D:(h + 1) * D, lanes], pc[slot, 0:2 * T, lanes]) * rs[slot, 0:1, lanes]
            at[h * D:(h + 1) * D, g * S + i * 2 * T:g * S + (i + 1) * 2 * T] = mixed.astype(BF16)

    groups = PP // G

    @pl.loop(0, B)
    def _(b):
        whole(b, sb1, rb1, ssem1, rsem1).wait_recv()
        mod = modb[b]
        arrived = rb1[b].astype(F32).reshape(n * R, C)
        for c in range(C // 128):
            zf[c] = arrived[:, c * 128:(c + 1) * 128]
        for g in range(groups):
            for i in range(G):
                rows = jnp.concatenate([zf[c, pl.ds(g * G + i, T, PP), :] for c in range(C // 128)], axis=1)
                tok[g, i * T:(i + 1) * T] = rows
                act[g, i * T:(i + 1) * T] = (rows + posb[...]).astype(BF16)
            project_qkv(g, w_qkv_t)
        staged([(g, h) for g in range(groups) for h in range(H)], temporal_score, temporal_soften, temporal_combine)
        branch = mm_tn(at[...], w_out_t[...])
        for g in range(groups):
            after = tok[g] + mod[2:3] * branch[g * S:(g + 1) * S]
            for i in range(G):
                for c in range(C // 128):
                    zf[c, pl.ds(g * G + i, T, PP), :] = after[i * T:(i + 1) * T, c * 128:(c + 1) * 128]
        leaving = jnp.concatenate([zf[c] for c in range(C // 128)], axis=1)
        sb2[b] = leaving.astype(BF16).reshape(n, R, C)
        send_all(b, sb2, rb2, ssem2, rsem2)

    for i in (7, 9, 10, 11):
        loads[i].wait()
    LP = kc.shape[1]

    @pl.loop(0, B)
    def _(b):
        whole(b, sb2, rb2, ssem2, rsem2).wait_recv()
        mod = modb[b]

        def cross_score(slot, f, h):
            sc[slot, 0:LP] = mm(kc[b, :, pair_lanes(h, D)], padded_head(qs.at[f], h, D, every))

        def cross_soften(slot, f, h):
            weights, inverse = weights_t(sc[slot, 0:L], scale)
            weights = jnp.concatenate([weights, jnp.zeros((LP - L, S), F32)], axis=0)
            pc[slot, 0:LP] = weights.astype(BF16)
            rs[slot] = jnp.broadcast_to(inverse, rs.shape[1:])

        def cross_combine(slot, f, h):
            mixed = mm(vc[b, h * D:(h + 1) * D], pc[slot, 0:LP]) * rs[slot, 0:1]
            at[h * D:(h + 1) * D, f * S:(f + 1) * S] = mixed.astype(BF16)

        hidden = rb2[b].astype(F32)
        for f in range(F):
            hid = hidden[:, f * PP:(f + 1) * PP, :].reshape(S, C)
            tok[f] = hid
            qs[f] = mm_nt(w_q_c[...], hid.astype(BF16)).astype(BF16)
        staged(units, cross_score, cross_soften, cross_combine)
        branch = mm_tn(at[...], w_out_c[...])
        for f in range(F):
            cross = (tok[f] + branch[f * S:(f + 1) * S]).astype(BF16).astype(F32)
            tok[f] = cross
            act[f] = (layer_norm(cross) * (1.0 + mod[4:5]) + mod[3:4]).astype(BF16)
        normed = act[...].reshape(F * S, C)
        wide = w_in.shape[1]
        for j in range(0, wide, 256):
            grown[:, j:j + 256] = gelu(mm(normed, w_in[:, j:j + 256])).astype(BF16)
        out = mm(grown[...], w_up[...])
        for f in range(F):
            yb[b, f] = (tok[f] + mod[5:6] * out[f * S:(f + 1) * S]).astype(BF16)
        pltpu.make_async_copy(yb.at[b], y_hbm.at[b], ysem.at[b]).start()

    @pl.loop(0, B)
    def _(b):
        pltpu.make_async_copy(yb.at[b], y_hbm.at[b], ysem.at[b]).wait()
        whole(b, sb1, rb1, ssem1, rsem1).wait_send()
        whole(b, sb2, rb2, ssem2, rsem2).wait_send()


def solution(mesh):
    n = mesh.shape['sp']
    act_spec = P('dp', 'sp', None, None)
    row_spec = P('dp', None, None)
    rep = [P(*[None] * k) for k in range(5)]
    in_specs = (act_spec, row_spec, row_spec, rep[2], rep[4], rep[3], rep[4], rep[3], rep[3], rep[4], rep[3], rep[2], rep[2])

    def local_block(latents, text_ctx, modulation, pos_temporal, w_qkv_spatial, w_out_spatial, w_qkv_temporal, w_out_temporal, w_query_cross, w_kv_cross, w_out_cross, w_mlp_in, w_mlp_out):
        B, F, S, C = latents.shape
        H, D, _ = w_out_spatial.shape
        L = text_ctx.shape[1]
        weights = [w.reshape(-1, w.shape[-1]) for w in (w_qkv_spatial, w_out_spatial, w_qkv_temporal, w_out_temporal, w_query_cross, w_kv_cross, w_out_cross, w_mlp_in, w_mlp_out)]
        args = [latents, text_ctx, modulation, pos_temporal] + weights
        R = F * (S // n)
        LP = -(-L // 16) * 16
        chunk = pltpu.VMEM((B, n, R, C), BF16)
        return pl.pallas_call(
            functools.partial(block_kernel, (n, B, F, S, C, H, D, L)),
            out_shape=jax.ShapeDtypeStruct(latents.shape, BF16),
            in_specs=[pl.BlockSpec(memory_space=pl.ANY)] * len(args),
            out_specs=pl.BlockSpec(memory_space=pl.ANY),
            scratch_shapes=[pltpu.VMEM(a.shape, a.dtype) for a in args] + [
                chunk, chunk, chunk, chunk,
                pltpu.VMEM((C // 128, n * R, 128), F32),
                pltpu.VMEM(latents.shape, BF16),
                pltpu.VMEM((B, LP, C), BF16),
                pltpu.VMEM((B, C, LP), BF16),
                pltpu.VMEM((F, C, S), BF16),
                pltpu.VMEM((F, S, C), BF16),
                pltpu.VMEM((F, C, S), BF16),
                pltpu.VMEM((C, F * S), BF16),
                pltpu.VMEM((DEPTH, S, S), F32),
                pltpu.VMEM((DEPTH, S, S), BF16),
                pltpu.VMEM((DEPTH, 8, S), F32),
                pltpu.VMEM((F, S, C), F32),
                pltpu.VMEM((F, S, C), BF16),
                pltpu.VMEM((F * S, w_mlp_in.shape[1]), BF16),
                pltpu.SemaphoreType.DMA((len(args) - 1,)),
                pltpu.SemaphoreType.DMA((B,)),
                pltpu.SemaphoreType.DMA((B,)),
                pltpu.SemaphoreType.DMA((B,)),
                pltpu.SemaphoreType.DMA((B,)),
                pltpu.SemaphoreType.DMA((B,)),
                pltpu.SemaphoreType.DMA((B,)),
            ],
            compiler_params=pltpu.CompilerParams(collective_id=0, has_side_effects=True, vmem_limit_bytes=60 * 1024 * 1024),
            name='st_block',
        )(*args)

    return jax.shard_map(local_block, mesh=mesh, in_specs=in_specs, out_specs=act_spec, check_vma=False)
```

time: 111 us -> 84.3 us (0.76)
  the two profiles are of different devices: /device:TPU:97 before, /device:TPU:99 now
where the time goes in v1:
time: 84.3 us; the launch traced here: 84.2 us
  Pallas kernels  80.9 us (96%)
  local copies, waits for them, and re-layouts  3.31 us (4%)
    pallas_call x1, Pallas kernels, local_block(): pl.pallas_call(functools.partial(block_kernel, (n, B, F, S, C, H, D, L)),...  80.9 us
    unnamed x1, local copies, waits for them, and re-layouts  3.31 us

profile of v1, /device:TPU:99, one launch (start us, length us, event | category | flops | bytes accessed | tf_op | source)
XLA Modules:
  0.0 84.2 jit_solution(3100195082203237125)
XLA Ops:
  0.0 80.9 %st_block.1 = bf16[6,2,256,384]{3,2,1,0:T(8,128)(2,1)} custom-call(bf16[6,2,256,384]{3,2,1,0:T(8,128)(2,1)} %x_hbm.1, bf16[6,120,384]{2,1,0:T(8,128)(2,1)} %ctx_hbm.1, f32[6,6,384]{2,1,0:T(8,128)} %mod_hbm.1, f32[64,384]{1,0:T(8,128)} %pos_hbm.1, bf16[1152,384]{1,0:T(8,128)(2,1)} %bitcast.7, bf16[384,384]{1,0:T(8,128)(2,1)} %bitcast.10, ...), custom_call_target="tpu_custom_call" | custom-call | tf_op jit(solution)/shard_map/st_block/pallas_call | solution.py:286
  80.9 3.3 %copy.15 = bf16[6,2,256,384]{3,2,1,0:T(8,128)(2,1)} copy(bf16[6,2,256,384]{3,2,1,0:T(8,128)(2,1)} %st_block.1) | data formatting | bytes 4718592

commit v2 on v1

--- a/solution.py
+++ b/solution.py
@@ -15,6 +15,7 @@
 BF16 = jnp.bfloat16
 MESH = pl.DeviceIdType.MESH
 DEPTH = 4
+VIDEOS = 2
 WEIGHTS = ('w_qkv_s', 'w_out_s', 'w_qkv_t', 'w_out_t', 'w_q_c', 'w_kv_c', 'w_out_c', 'w_in', 'w_up')
 
 
@@ -68,10 +69,26 @@
             combine((i - 2) % DEPTH, *units[i - 2])
 
 
+def send_order(n):
+    side = max(k for k in range(1, n) if (n // 2) % k == 0 and k * k <= n // 2)
+    rows = n // 2 // side
+    lists = []
+    for turn, dx in enumerate([1 % side, side - 1] + [k for k in range(side) if k not in (1 % side, side - 1)]):
+        steps = [(dy + turn) % rows for dy in range(rows)]
+        lists.append([(dy, dx, dc) for dc in range(2) for dy in steps])
+    if side == 1:
+        lists = lists[:1]
+    longest = max(len(part) for part in lists)
+    order = [part[i] for i in range(longest) for part in lists if i < len(part)]
+    order = list(dict.fromkeys(order))
+    return side, [offset for offset in order if offset != (0, 0, 0)]
+
+
 def block_kernel(cfg, x_hbm, ctx_hbm, mod_hbm, pos_hbm, *rest):
     n, B, F, S, C, H, D, L = cfg
     PP = S // n
     T = F * n
+    V = VIDEOS if B % VIDEOS == 0 else 1
     R = F * PP
     NW = len(WEIGHTS)
     w_hbm = rest[:NW]
@@ -82,6 +99,14 @@
     w_qkv_s, w_out_s, w_qkv_t, w_out_t, w_q_c, w_kv_c, w_out_c, w_in, w_up = wv
     scale = D ** -0.5
     me = lax.axis_index('sp')
+    side, order = send_order(n)
+
+    def peer_of(offset):
+        dy, dx, dc = offset
+        x = lax.rem(me // 2, side)
+        y = me // (2 * side)
+        return (lax.rem(y + dy, n // (2 * side)) * side + lax.rem(x + dx, side)) * 2 + lax.rem(me + dc, 2)
+
 
     def x_copy(b):
         return pltpu.make_async_copy(x_hbm.at[b], xb.at[b], xsem.at[b])
@@ -103,22 +128,18 @@
     def _(j):
         pl.semaphore_signal(barrier, inc=1, device_id={'sp': lax.rem(me + j, n)}, device_id_type=MESH)
 
-    pl.semaphore_wait(barrier, n - 1)
-
-    def send_all(b, sbuf, rbuf, ssem, rsem):
-        rbuf[b, me] = sbuf[b, me]
-
-        @pl.loop(1, n)
-        def _(j):
-            peer = lax.rem(me + j, n)
+    def send_all(g, sbuf, rbuf, ssem, rsem):
+        rbuf[g, me] = sbuf[g, me]
+        for offset in order:
+            peer = peer_of(offset)
             pltpu.make_async_remote_copy(
-                src_ref=sbuf.at[b, peer], dst_ref=rbuf.at[b, me], send_sem=ssem.at[b], recv_sem=rsem.at[b],
+                src_ref=sbuf.at[g, peer], dst_ref=rbuf.at[g, me], send_sem=ssem.at[g], recv_sem=rsem.at[g],
                 device_id={'sp': peer}, device_id_type=MESH).start()
 
-    def whole(b, sbuf, rbuf, ssem, rsem):
+    def whole(g, sbuf, rbuf, ssem, rsem):
         return pltpu.make_async_remote_copy(
-            src_ref=sbuf.at[b, pl.ds(0, n - 1)], dst_ref=rbuf.at[b, pl.ds(0, n - 1)], send_sem=ssem.at[b],
-            recv_sem=rsem.at[b], device_id={'sp': me}, device_id_type=MESH)
+            src_ref=sbuf.at[g, pl.ds(0, n - 1)], dst_ref=rbuf.at[g, pl.ds(0, n - 1)], send_sem=ssem.at[g],
+            recv_sem=rsem.at[g], device_id={'sp': me}, device_id_type=MESH)
 
     def project_qkv(i, w_ref):
         acts = act[i]
@@ -146,8 +167,8 @@
 
     units = [(f, h) for f in range(F) for h in range(H)]
 
-    @pl.loop(0, B)
-    def _(b):
+    def spatial(g, i):
+        b = g * V + i
         x_copy(b).wait()
         mod = modb[b]
         for f in range(F):
@@ -156,8 +177,17 @@
         staged(units, spatial_score, spatial_soften, spatial_combine)
         branch = mm_tn(at[...], w_out_s[...])
         outs = [(xb[b, f].astype(F32) + mod[2:3] * branch[f * S:(f + 1) * S]).reshape(n, PP, C) for f in range(F)]
-        sb1[b] = jnp.concatenate(outs, axis=1).astype(BF16)
-        send_all(b, sb1, rb1, ssem1, rsem1)
+        sb1[g, :, i] = jnp.concatenate(outs, axis=1).astype(BF16)
+
+    @pl.loop(0, B // V)
+    def _(g):
+        pl.loop(0, V)(functools.partial(spatial, g))
+
+        @pl.when(g == 0)
+        def _():
+            pl.semaphore_wait(barrier, n - 1)
+
+        send_all(g, sb1, rb1, ssem1, rsem1)
 
     loads[0].wait()
     loads[8].wait()
@@ -194,11 +224,10 @@
 
     groups = PP // G
 
-    @pl.loop(0, B)
-    def _(b):
-        whole(b, sb1, rb1, ssem1, rsem1).wait_recv()
+    def temporal(grp, vid):
+        b = grp * V + vid
         mod = modb[b]
-        arrived = rb1[b].astype(F32).reshape(n * R, C)
+        arrived = rb1[grp, :, vid].astype(F32).reshape(n * R, C)
         for c in range(C // 128):
             zf[c] = arrived[:, c * 128:(c + 1) * 128]
         for g in range(groups):
@@ -215,16 +244,20 @@
                 for c in range(C // 128):
                     zf[c, pl.ds(g * G + i, T, PP), :] = after[i * T:(i + 1) * T, c * 128:(c + 1) * 128]
         leaving = jnp.concatenate([zf[c] for c in range(C // 128)], axis=1)
-        sb2[b] = leaving.astype(BF16).reshape(n, R, C)
-        send_all(b, sb2, rb2, ssem2, rsem2)
+        sb2[grp, :, vid] = leaving.astype(BF16).reshape(n, R, C)
+
+    @pl.loop(0, B // V)
+    def _(grp):
+        whole(grp, sb1, rb1, ssem1, rsem1).wait_recv()
+        pl.loop(0, V)(functools.partial(temporal, grp))
+        send_all(grp, sb2, rb2, ssem2, rsem2)
 
     for i in (7, 9, 10, 11):
         loads[i].wait()
     LP = kc.shape[1]
 
-    @pl.loop(0, B)
-    def _(b):
-        whole(b, sb2, rb2, ssem2, rsem2).wait_recv()
+    def final(grp, vid):
+        b = grp * V + vid
         mod = modb[b]
 
         def cross_score(slot, f, h):
@@ -240,7 +273,7 @@
             mixed = mm(vc[b, h * D:(h + 1) * D], pc[slot, 0:LP]) * rs[slot, 0:1]
             at[h * D:(h + 1) * D, f * S:(f + 1) * S] = mixed.astype(BF16)
 
-        hidden = rb2[b].astype(F32)
+        hidden = rb2[grp, :, vid].astype(F32)
         for f in range(F):
             hid = hidden[:, f * PP:(f + 1) * PP, :].reshape(S, C)
             tok[f] = hid
@@ -260,11 +293,19 @@
             yb[b, f] = (tok[f] + mod[5:6] * out[f * S:(f + 1) * S]).astype(BF16)
         pltpu.make_async_copy(yb.at[b], y_hbm.at[b], ysem.at[b]).start()
 
+    @pl.loop(0, B // V)
+    def _(grp):
+        whole(grp, sb2, rb2, ssem2, rsem2).wait_recv()
+        pl.loop(0, V)(functools.partial(final, grp))
+
     @pl.loop(0, B)
     def _(b):
         pltpu.make_async_copy(yb.at[b], y_hbm.at[b], ysem.at[b]).wait()
-        whole(b, sb1, rb1, ssem1, rsem1).wait_send()
-        whole(b, sb2, rb2, ssem2, rsem2).wait_send()
+
+    @pl.loop(0, B // V)
+    def _(g):
+        whole(g, sb1, rb1, ssem1, rsem1).wait_send()
+        whole(g, sb2, rb2, ssem2, rsem2).wait_send()
 
 
 def solution(mesh):
@@ -282,7 +323,8 @@
         args = [latents, text_ctx, modulation, pos_temporal] + weights
         R = F * (S // n)
         LP = -(-L // 16) * 16
-        chunk = pltpu.VMEM((B, n, R, C), BF16)
+        V = VIDEOS if B % VIDEOS == 0 else 1
+        chunk = pltpu.VMEM((B // V, n, V, R, C), BF16)
         return pl.pallas_call(
             functools.partial(block_kernel, (n, B, F, S, C, H, D, L)),
             out_shape=jax.ShapeDtypeStruct(latents.shape, BF16),
@@ -307,10 +349,10 @@
                 pltpu.SemaphoreType.DMA((len(args) - 1,)),
                 pltpu.SemaphoreType.DMA((B,)),
                 pltpu.SemaphoreType.DMA((B,)),
-                pltpu.SemaphoreType.DMA((B,)),
-                pltpu.SemaphoreType.DMA((B,)),
-                pltpu.SemaphoreType.DMA((B,)),
-                pltpu.SemaphoreType.DMA((B,)),
+                pltpu.SemaphoreType.DMA((B // V,)),
+                pltpu.SemaphoreType.DMA((B // V,)),
+                pltpu.SemaphoreType.DMA((B // V,)),
+                pltpu.SemaphoreType.DMA((B // V,)),
             ],
             compiler_params=pltpu.CompilerParams(collective_id=0, has_side_effects=True, vmem_limit_bytes=60 * 1024 * 1024),
             name='st_block',

time: 84.3 us -> 88.8 us (1.053)
  the two profiles are of different devices: /device:TPU:99 before, /device:TPU:97 now
where the time goes in v2:
time: 88.8 us; the launch traced here: 88.7 us
  Pallas kernels  85.4 us (96%)
  local copies, waits for them, and re-layouts  3.31 us (4%)
    pallas_call x1, Pallas kernels, local_block(): pl.pallas_call(functools.partial(block_kernel, (n, B, F, S, C, H, D, L)),...  85.4 us
    unnamed x1, local copies, waits for them, and re-layouts  3.31 us

profile of v2, /device:TPU:97, one launch (start us, length us, event | category | flops | bytes accessed | tf_op | source)
XLA Modules:
  0.0 88.7 jit_solution(16787089143862567464)
XLA Ops:
  0.0 85.4 %st_block.1 = bf16[6,2,256,384]{3,2,1,0:T(8,128)(2,1)} custom-call(bf16[6,2,256,384]{3,2,1,0:T(8,128)(2,1)} %x_hbm.1, bf16[6,120,384]{2,1,0:T(8,128)(2,1)} %ctx_hbm.1, f32[6,6,384]{2,1,0:T(8,128)} %mod_hbm.1, f32[64,384]{1,0:T(8,128)} %pos_hbm.1, bf16[1152,384]{1,0:T(8,128)(2,1)} %bitcast.7, bf16[384,384]{1,0:T(8,128)(2,1)} %bitcast.10, ...), custom_call_target="tpu_custom_call" | custom-call | tf_op jit(solution)/shard_map/st_block/pallas_call | solution.py:328
  85.4 3.3 %copy.15 = bf16[6,2,256,384]{3,2,1,0:T(8,128)(2,1)} copy(bf16[6,2,256,384]{3,2,1,0:T(8,128)(2,1)} %st_block.1) | data formatting | bytes 4718592
